TPU v7x, 32 devices: a whole 2x2x4 slice. The times are simulated.
32 devices in a mesh: expert: 4 (over y, x), shard: 8 (over z, core).
Axes of the slice: x: 2, y: 2, z: 4, core: 2. Of those that a mesh axis runs over, the one named last changes fastest.
Arguments:
- master_gate: float32 [64, 2048, 1408], P('expert', 'shard'), may hold values from -0.1875 to 0.1875
- master_up: float32 [64, 2048, 1408], P('expert', 'shard'), may hold values from -0.1875 to 0.1875
- master_down: float32 [64, 1408, 2048], P('expert', None, 'shard'), may hold values from -0.21875 to 0.21875
- router_weight: float32 [2048, 64], P('shard', 'expert'), may hold values from -0.125 to 0.125
- router_gain: float32 [2048], P('shard'), may hold values from 0.25 to 1.75
Outputs:
- final_gate: bfloat16 [64, 2048, 1408], P('expert', None, 'shard')
- final_up: bfloat16 [64, 2048, 1408], P('expert', None, 'shard')
- final_down: bfloat16 [64, 1408, 2048], P('expert', 'shard')
- scale_gate: float32 [64, 1408], P('expert', 'shard')
- scale_up: float32 [64, 1408], P('expert', 'shard')
- scale_down: float32 [64, 1408], P('expert', 'shard')
- serve_router: bfloat16 [2048, 64], replicated
All inputs are finite; a program needn't handle non-finite values. Where the computation divides by a largest or mean magnitude, that divisor is 1e-20 or more.
Results may differ from a plain program's by a relative error of at most 0.001.
Values may be sent and summed in bfloat16 or wider, within the bound.
A program may use at most 256 MiB of HBM per device.

v0:
```python
import functools

import jax
import jax.numpy as jnp
from jax import lax
from jax.experimental import pallas as pl
from jax.experimental.pallas import tpu as pltpu
from jax.sharding import PartitionSpec as P

MESH = pl.DeviceIdType.MESH
LANES = 128
PAIR = 2


def kernel(
    n, groups_of_experts, gate, up, down, weight, gain,
    out_gate, out_up, out_down, scales, router,
    wide_max, tall_max, wide, tall, turned, column, stage, local, got, kept, part, rows,
    load_max, load_bulk, msg_send, msg_recv, bulk_send, bulk_recv, own_sem, router_sem,
):
    me = lax.axis_index("shard")
    team = lax.axis_index("expert")
    experts, depth, inner = gate.shape
    block = inner // n
    per_array = experts // PAIR
    total = 3 * per_array
    wide_groups = 2 * per_array
    bits = n.bit_length() - 1
    steps = bits + 1
    ins, outs = (gate, up, down), (out_gate, out_up, out_down)
    core = lax.rem(me, 2)

    def partner(step):
        size = 1 if step == steps - 1 else 2**step
        return me + (1 - 2 * lax.rem(me // size, 2)) * size

    barrier = pltpu.get_barrier_semaphore()
    for d in range(1, n):
        pl.semaphore_signal(barrier, inc=1, device_id={"shard": lax.rem(me + d, n)}, device_id_type=MESH)
    for d in range(1, groups_of_experts):
        pl.semaphore_signal(
            barrier, inc=1, device_id={"expert": lax.rem(team + d, groups_of_experts)}, device_id_type=MESH
        )

    def load(group, wide_buf, tall_buf, sem, act):
        for m in range(3):

            @pl.when(group // per_array == m)
            def _():
                first = lax.rem(group, per_array) * PAIR
                act(pltpu.make_async_copy(ins[m].at[pl.ds(first, PAIR)], tall_buf if m == 2 else wide_buf, sem))

    load(0, wide_max, tall_max, load_max, lambda c: c.start())
    load(0, wide, tall, load_bulk, lambda c: c.start())
    pl.semaphore_wait(barrier, n + groups_of_experts - 2)

    team_rows = pl.ds(pl.multiple_of(team * part.shape[0], part.shape[0]), part.shape[0])
    my_columns = pl.ds(pl.multiple_of(me * depth, depth), depth)
    product = (weight[...] * gain[...]).astype(jnp.bfloat16)
    part[...] = product
    rows[team_rows, my_columns] = product
    for d in range(1, n):
        pltpu.make_async_remote_copy(
            part, rows.at[team_rows, my_columns], router_sem.at[0], router_sem.at[1],
            device_id={"shard": lax.rem(me + d, n)}, device_id_type=MESH,
        ).start()
    router_bytes = rows.at[pl.ds(0, part.shape[0]), pl.ds(0, (n - 1) * depth)]
    team_bytes = rows.at[pl.ds(0, (groups_of_experts - 1) * part.shape[0])]

    def message(step, group):
        source = local.at[group * PAIR + 1 - core] if step == 0 else kept.at[step, group]
        return pltpu.make_async_remote_copy(
            source, got.at[step, group], msg_send.at[step, group], msg_recv.at[step, group],
            device_id={"shard": partner(step)}, device_id_type=MESH,
        )

    def local_max(group):
        load(group, wide_max, tall_max, load_max, lambda c: c.wait())

        @pl.when(group < wide_groups)
        def _():
            for j in range(PAIR):
                for b in range(inner // LANES):
                    lanes = pl.ds(b * LANES, LANES)
                    local[group * PAIR + j, :, lanes] = jnp.max(jnp.abs(wide_max[j, :, lanes]), axis=0, keepdims=True)

        @pl.when(group >= wide_groups)
        def _():
            for j in range(PAIR):
                for b in range(inner // LANES):
                    lanes = pl.ds(b * LANES, LANES)
                    most = jnp.abs(tall_max[j, lanes, pl.ds(0, LANES)])
                    for h in range(1, depth // LANES):
                        most = jnp.maximum(most, jnp.abs(tall_max[j, lanes, pl.ds(h * LANES, LANES)]))
                    local[group * PAIR + j, :, lanes] = jnp.max(most.T, axis=0, keepdims=True)

        @pl.when(group + 1 < total)
        def _():
            load(group + 1, wide_max, tall_max, load_max, lambda c: c.start())

        message(0, group).start()

    def reduce_step(step, group):
        message(step - 1, group).wait_recv()
        held = local[group * PAIR + core] if step == 1 else kept[step - 1, group]
        most = jnp.maximum(held, got[step - 1, group])
        kept[step, group] = most
        if step == steps - 1:
            scales[group * PAIR + core] = most
        message(step, group).start()

    def normalise(j, source, chunk):
        for p in range(n):
            part_rows = pl.ds(p * block, block)
            for h in range(depth // LANES):
                lanes = pl.ds(h * LANES, LANES)
                x = source[part_rows, lanes] if j is None else source[j, part_rows, lanes]
                stage[chunk, p, :, lanes] = (x / column[part_rows]).astype(jnp.bfloat16)

    def bulk(group):
        message(steps - 1, group).wait_recv()
        scales[group * PAIR + 1 - core] = got[steps - 1, group]
        load(group, wide, tall, load_bulk, lambda c: c.wait())

        @pl.loop(0, PAIR)
        def _(j):
            chunk = group * PAIR + j
            for b in range(inner // LANES):
                lanes = pl.ds(b * LANES, LANES)
                column[lanes] = jnp.broadcast_to(scales[chunk, :, lanes], (LANES, LANES)).T

            @pl.when(group < wide_groups)
            def _():
                for b in range(inner // LANES):
                    lanes = pl.ds(b * LANES, LANES)
                    for h in range(depth // LANES):
                        half = pl.ds(h * LANES, LANES)
                        turned[lanes, half] = wide[j, half, lanes].T
                normalise(None, turned, chunk)

            @pl.when(group >= wide_groups)
            def _():
                normalise(j, tall, chunk)

            for m in range(3):

                @pl.when(group // per_array == m)
                def _():
                    place = outs[m].at[chunk - m * experts, :, my_columns]
                    for d in range(n):
                        p = lax.rem(me + n // 2 + d, n)
                        if d == n // 2:
                            pltpu.make_async_copy(stage.at[chunk, me], place, own_sem.at[m]).start()
                        else:
                            pltpu.make_async_remote_copy(
                                stage.at[chunk, p], place, bulk_send.at[m], bulk_recv.at[m],
                                device_id={"shard": p}, device_id_type=MESH,
                            ).start()

        @pl.when(group + 1 < total)
        def _():
            load(group + 1, wide, tall, load_bulk, lambda c: c.start())

    @pl.loop(0, total + steps)
    def _(t):
        for step in reversed(range(1, steps)):

            @pl.when((t >= step) & (t < total + step))
            def _():
                reduce_step(step, t - step)

        @pl.when(t < total)
        def _():
            local_max(t)

        @pl.when(t == 1)
        def _():
            pltpu.make_async_copy(router_bytes, router_bytes, router_sem.at[1]).wait()
            for d in range(1, groups_of_experts):
                pltpu.make_async_remote_copy(
                    rows.at[team_rows], rows.at[team_rows], router_sem.at[2], router_sem.at[3],
                    device_id={"expert": lax.rem(team + d, groups_of_experts)}, device_id_type=MESH,
                ).start()

        @pl.when(t >= steps)
        def _():
            bulk(t - steps)

    pltpu.make_async_copy(router_bytes, router_bytes, router_sem.at[0]).wait()
    for s in (2, 3):
        pltpu.make_async_copy(team_bytes, team_bytes, router_sem.at[s]).wait()
    router[...] = rows[...]

    @pl.loop(0, total)
    def _(group):
        for step in range(steps):
            message(step, group).wait_send()

    for m in range(3):
        sent = outs[m].at[:, :, pl.ds(0, (n - 1) * depth)]
        own = outs[m].at[:, :, pl.ds(0, depth)]
        pltpu.make_async_copy(own, own, own_sem.at[m]).wait()
        pltpu.make_async_copy(sent, sent, bulk_send.at[m]).wait()
        pltpu.make_async_copy(sent, sent, bulk_recv.at[m]).wait()


def plain(master_gate, master_up, master_down, router_weight, router_gain):
    scale_gate, scale_up, scale_down = lax.pmax(
        (
            jnp.max(jnp.abs(master_gate), axis=1),
            jnp.max(jnp.abs(master_up), axis=1),
            jnp.max(jnp.abs(master_down), axis=2),
        ),
        "shard",
    )
    narrow_gate, narrow_up, narrow_down = (
        (master_gate / jnp.expand_dims(scale_gate, 1)).astype(jnp.bfloat16),
        (master_up / jnp.expand_dims(scale_up, 1)).astype(jnp.bfloat16),
        (master_down / jnp.expand_dims(scale_down, 2)).astype(jnp.bfloat16),
    )
    final_gate, final_up = (
        lax.all_to_all(narrow_gate, "shard", split_axis=2, concat_axis=1, tiled=True),
        lax.all_to_all(narrow_up, "shard", split_axis=2, concat_axis=1, tiled=True),
    )
    final_down = lax.all_to_all(narrow_down, "shard", split_axis=1, concat_axis=2, tiled=True)
    scale_gate = lax.dynamic_slice_in_dim(
        scale_gate, lax.axis_index("shard") * final_gate.shape[2], final_gate.shape[2], axis=1
    )
    scale_up = lax.dynamic_slice_in_dim(
        scale_up, lax.axis_index("shard") * final_up.shape[2], final_up.shape[2], axis=1
    )
    scale_down = lax.dynamic_slice_in_dim(
        scale_down, lax.axis_index("shard") * final_down.shape[1], final_down.shape[1], axis=1
    )
    part_router = (router_weight * router_gain[:, None]).astype(jnp.bfloat16)
    row_router = lax.all_gather(part_router, "shard", axis=0, tiled=True)
    serve_router = lax.all_gather(row_router, "expert", axis=1, tiled=True)
    return (final_gate, final_up, final_down, scale_gate, scale_up, scale_down, serve_router)


def solution(mesh):
    n, teams = mesh.shape["shard"], mesh.shape["expert"]

    def body(master_gate, master_up, master_down, router_weight, router_gain):
        experts, depth, inner = master_gate.shape
        block = inner // n
        chunks = 3 * experts
        groups = chunks // PAIR
        steps = n.bit_length()
        columns = router_weight.shape[1]
        fits = depth % LANES == 0 and inner % LANES == 0 and block % 8 == 0
        if n < 4 or n & (n - 1) or experts % PAIR or not fits:
            return plain(master_gate, master_up, master_down, router_weight, router_gain)
        f32, bf16 = jnp.float32, jnp.bfloat16
        dma = pltpu.SemaphoreType.DMA
        final = jax.ShapeDtypeStruct((experts, block, n * depth), bf16)
        hbm, vmem = pl.BlockSpec(memory_space=pl.ANY), pl.BlockSpec(memory_space=pltpu.VMEM)
        gate, up, down, scales, router = pl.pallas_call(
            functools.partial(kernel, n, teams),
            out_shape=(
                final, final, final,
                jax.ShapeDtypeStruct((chunks, 1, inner), f32),
                jax.ShapeDtypeStruct((teams * columns, n * depth), bf16),
            ),
            in_specs=[hbm, hbm, hbm, vmem, vmem],
            out_specs=(hbm, hbm, hbm, vmem, vmem),
            scratch_shapes=[
                pltpu.VMEM((PAIR, depth, inner), f32),
                pltpu.VMEM((PAIR, inner, depth), f32),
                pltpu.VMEM((PAIR, depth, inner), f32),
                pltpu.VMEM((PAIR, inner, depth), f32),
                pltpu.VMEM((inner, depth), f32),
                pltpu.VMEM((inner, LANES), f32),
                pltpu.VMEM((chunks, n, block, depth), bf16),
                pltpu.VMEM((chunks, 1, inner), f32),
                pltpu.VMEM((steps, groups, 1, inner), f32),
                pltpu.VMEM((steps, groups, 1, inner), f32),
                pltpu.VMEM((columns, depth), bf16),
                pltpu.VMEM((teams * columns, n * depth), bf16),
                dma, dma,
                dma((steps, groups)), dma((steps, groups)),
                dma((3,)), dma((3,)), dma((3,)), dma((4,)),
            ],
            compiler_params=pltpu.CompilerParams(
                collective_id=0, has_side_effects=True, vmem_limit_bytes=62 * 1024 * 1024
            ),
        )(master_gate, master_up, master_down, router_weight.T, router_gain[None, :])
        mine = lax.dynamic_slice_in_dim(
            scales.reshape(3, experts, inner), lax.axis_index("shard") * block, block, axis=2
        )
        return (gate.swapaxes(1, 2), up.swapaxes(1, 2), down, mine[0], mine[1], mine[2], router.T)

    return jax.shard_map(
        body,
        mesh=mesh,
        in_specs=(
            P("expert", "shard", None),
            P("expert", "shard", None),
            P("expert", None, "shard"),
            P("shard", "expert"),
            P("shard"),
        ),
        out_specs=(
            P("expert", None, "shard"),
            P("expert", None, "shard"),
            P("expert", "shard", None),
            P("expert", "shard"),
            P("expert", "shard"),
            P("expert", "shard"),
            P(),
        ),
        check_vma=False,
    )
```

profile of v0, /device:TPU:0, one launch (start us, length us, event | category | flops | bytes accessed | tf_op | source)
XLA Modules:
  0.0 793.1 jit_solution(17037276164366188370)
XLA Ops:
  0.6 766.1 %shard_map.108 = (bf16[16,176,2048]{2,1,0:T(8,128)(2,1)}, bf16[16,176,2048]{2,1,0:T(8,128)(2,1)}, bf16[16,176,2048]{2,1,0:T(8,128)(2,1)}, f32[48,1,1408]{2,1,0:T(1,128)}, bf16[64,2048]{1,0:T(8,128)(2,1)}) custom-call(f32[16,256,1408]{2,1,0:T(8,128)} %gate.1, f32[16,256,1408]{2,1,0:T(8,128)} %up.1, f32[16,1408,256]{2,1,0:T(8,128)} %down.1, ...), custom_call_target="tpu_custom_call" | custom-call | tf_op jit(solution)/shard_map/pallas_call | solution.py:258
  766.7 1.0 copy.12
  767.7 0.7 dynamic-slice_bitcast_fusion
  768.4 0.0 copy-start
  768.4 0.0 slice-start
  768.4 0.0 slice-start.1
  768.4 12.0 %copy.17 = bf16[16,2048,176]{1,2,0:T(8,128)(2,1)} copy(bf16[16,2048,176]{1,2,0:T(8,128)(2,1)} %bitcast.15) | data formatting | bytes 23068672
  780.4 0.0 copy-done
  780.4 0.0 slice-start.2
  780.4 5.8 copy.18
  786.2 0.0 slice-done
  786.2 0.0 slice-done.1
  786.2 1.7 slice-done.2
  788.0 0.0 copy-start.1
  788.0 4.4 copy.19
  792.4 0.0 copy-done.1
  792.4 0.7 copy.20
  (1 shorter events, 0.0 us)
Async XLA Ops:
  768.4 12.0 %copy-start = (bf16[16,176,2048]{2,1,0:T(8,128)(2,1)S(1)}, bf16[16,176,2048]{2,1,0:T(8,128)(2,1)}, u32[]{:S(2)}) copy-start(bf16[16,176,2048]{2,1,0:T(8,128)(2,1)} %get-tuple-element.13) | copy-start | bytes 34603012
  768.4 17.8 %slice-start = ((s8[11534336]{0:T(1024)(128)(4,1)}), s8[4194304]{0:T(1024)(128)(4,1)S(1)}, s32[]{:S(2)}) async-start(s8[11534336]{0:T(1024)(128)(4,1)} %bitcast.12), calls=%async_computation | async-start | bytes 8388608
  768.4 17.8 %slice-start.1 = ((s8[11534336]{0:T(1024)(128)(4,1)}), s8[4194304]{0:T(1024)(128)(4,1)S(1)}, s32[]{:S(2)}) async-start(s8[11534336]{0:T(1024)(128)(4,1)} %bitcast.12), calls=%async_computation.1 | async-start | bytes 8388608
  780.4 7.6 slice-start.2
  788.0 4.4 copy-start.1
where the time goes:
time: 793 us
  Pallas kernels  766 us (97%)
  local copies, waits for them, and re-layouts  26.4 us (3%)
    pallas_call x1, Pallas kernels, body(): pl.pallas_call(functools.partial(kernel, n, teams), out_shape=(final, fin...  766 us
    unnamed x15, local copies, waits for them, and re-layouts  25.7 us

commit v1 on v0

--- a/solution.py
+++ b/solution.py
@@ -10,13 +10,22 @@
 MESH = pl.DeviceIdType.MESH
 LANES = 128
 PAIR = 2
+CORES = 2
+HELD_SHARE = 6
+LEAD = 2
+
+
+def across(n, me):
+    half = n // 2
+    return [(1 - me // half) * half + lax.rem(me, CORES) + CORES * q for q in range(half // CORES)]
 
 
 def kernel(
     n, groups_of_experts, gate, up, down, weight, gain,
-    out_gate, out_up, out_down, scales, router,
+    out_gate, out_up, out_down, scales, router, later,
     wide_max, tall_max, wide, tall, turned, column, stage, local, got, kept, part, rows,
-    load_max, load_bulk, msg_send, msg_recv, bulk_send, bulk_recv, own_sem, router_sem,
+    load_max, load_bulk, msg_send, msg_recv, bulk_send, bulk_recv, own_sem, router_sem, later_sem,
+    first, first_send, first_recv, turn,
 ):
     me = lax.axis_index("shard")
     team = lax.axis_index("expert")
@@ -24,15 +33,23 @@
     block = inner // n
     per_array = experts // PAIR
     total = 3 * per_array
+    direct = LEAD * PAIR
     wide_groups = 2 * per_array
     bits = n.bit_length() - 1
-    steps = bits + 1
+    cross, share, last = bits - 1, bits, bits + 1
+    steps = bits + 2
     ins, outs = (gate, up, down), (out_gate, out_up, out_down)
-    core = lax.rem(me, 2)
+    core = lax.rem(me, CORES)
+    half = n // 2
+    held = later.shape[0]
+    first_held = 3 * experts - held
 
     def partner(step):
-        size = 1 if step == steps - 1 else 2**step
+        size = {share: CORES, last: 1}.get(step, 2**step)
         return me + (1 - 2 * lax.rem(me // size, 2)) * size
+
+    def crosses(group):
+        return lax.rem(me // CORES, 2) == lax.rem(group, 2)
 
     barrier = pltpu.get_barrier_semaphore()
     for d in range(1, n):
@@ -50,9 +67,37 @@
                 first = lax.rem(group, per_array) * PAIR
                 act(pltpu.make_async_copy(ins[m].at[pl.ds(first, PAIR)], tall_buf if m == 2 else wide_buf, sem))
 
-    load(0, wide_max, tall_max, load_max, lambda c: c.start())
     load(0, wide, tall, load_bulk, lambda c: c.start())
+    load(1, wide_max, tall_max, load_max, lambda c: c.start())
+
+    def first_max(source, j, chunk):
+        for b in range(inner // LANES):
+            lanes = pl.ds(b * LANES, LANES)
+            first[me, chunk, :, lanes] = jnp.max(jnp.abs(source[j, :, lanes]), axis=0, keepdims=True)
+
+    def first_message(k, d):
+        own = first.at[me, pl.ds(k, 1 if k == 0 else direct - 1)]
+        return pltpu.make_async_remote_copy(
+            own, own, first_send.at[k], first_recv.at[k],
+            device_id={"shard": lax.rem(me + d, n)}, device_id_type=MESH,
+        )
+
+    def first_bytes(k):
+        return first.at[pl.ds(0, n - 1), pl.ds(k, 1 if k == 0 else direct - 1)]
+
+    load(0, wide, tall, load_bulk, lambda c: c.wait())
+    first_max(wide, 0, 0)
     pl.semaphore_wait(barrier, n + groups_of_experts - 2)
+    for d in range(1, n):
+        first_message(0, d).start()
+    for j in range(1, PAIR):
+        first_max(wide, j, j)
+    load(1, wide_max, tall_max, load_max, lambda c: c.wait())
+    for j in range(PAIR):
+        first_max(wide_max, j, PAIR + j)
+    load(LEAD, wide_max, tall_max, load_max, lambda c: c.start())
+    for d in range(1, n):
+        first_message(1, d).start()
 
     team_rows = pl.ds(pl.multiple_of(team * part.shape[0], part.shape[0]), part.shape[0])
     my_columns = pl.ds(pl.multiple_of(me * depth, depth), depth)
@@ -101,71 +146,151 @@
         message(0, group).start()
 
     def reduce_step(step, group):
-        message(step - 1, group).wait_recv()
-        held = local[group * PAIR + core] if step == 1 else kept[step - 1, group]
-        most = jnp.maximum(held, got[step - 1, group])
-        kept[step, group] = most
-        if step == steps - 1:
-            scales[group * PAIR + core] = most
-        message(step, group).start()
-
-    def normalise(j, source, chunk):
-        for p in range(n):
-            part_rows = pl.ds(p * block, block)
+        if step < share:
+            message(step - 1, group).wait_recv()
+            held = local[group * PAIR + core] if step == 1 else kept[step - 1, group]
+            kept[step, group] = jnp.maximum(held, got[step - 1, group])
+            if step < cross:
+                message(step, group).start()
+                return
+
+        @pl.when(crosses(group))
+        def _():
+            if step == share:
+                message(cross, group).wait_recv()
+                kept[share, group] = jnp.maximum(kept[cross, group], got[cross, group])
+            if step == last:
+                kept[last, group] = kept[share, group]
+            else:
+                message(step, group).start()
+
+        if step == last:
+
+            @pl.when(jnp.logical_not(crosses(group)))
+            def _():
+                message(share, group).wait_recv()
+                kept[last, group] = got[share, group]
+
+            scales[group * PAIR + core] = kept[last, group]
+            message(last, group).start()
+
+    def normalise(j, source, chunk, p):
+        part_rows = pl.ds(p * block if isinstance(p, int) else pl.multiple_of(p * block, 8), block)
+        for h in range(depth // LANES):
+            lanes = pl.ds(h * LANES, LANES)
+            x = source[part_rows, lanes] if j is None else source[j, part_rows, lanes]
+            stage[chunk, p, :, lanes] = (x / column[part_rows]).astype(jnp.bfloat16)
+
+    def spread(chunk):
+        for b in range(inner // LANES):
+            lanes = pl.ds(b * LANES, LANES)
+            column[lanes] = jnp.broadcast_to(scales[chunk, :, lanes], (LANES, LANES)).T
+
+    def turn_over(j):
+        for b in range(inner // LANES):
+            lanes = pl.ds(b * LANES, LANES)
             for h in range(depth // LANES):
-                lanes = pl.ds(h * LANES, LANES)
-                x = source[part_rows, lanes] if j is None else source[j, part_rows, lanes]
-                stage[chunk, p, :, lanes] = (x / column[part_rows]).astype(jnp.bfloat16)
+                part = pl.ds(h * LANES, LANES)
+                turned[lanes, part] = wide[j, part, lanes].T
+
+    def keep(chunk, m):
+        pltpu.make_async_copy(
+            stage.at[chunk, me], outs[m].at[chunk - m * experts, :, my_columns], own_sem.at[m]
+        ).start()
+
+    def first_bulk(chunk):
+        j = lax.rem(chunk, PAIR)
+
+        @pl.when((chunk > 0) & (j == 0))
+        def _():
+            load(chunk // PAIR, wide, tall, load_bulk, lambda c: c.wait())
+
+        turn_over(j)
+        for k in range(2):
+
+            @pl.when(chunk == k)
+            def _():
+                pltpu.make_async_copy(first_bytes(k), first_bytes(k), first_recv.at[k]).wait()
+
+        for b in range(inner // LANES):
+            lanes = pl.ds(b * LANES, LANES)
+            scales[chunk, :, lanes] = jnp.max(first[:, chunk, :, lanes], axis=0)
+        spread(chunk)
+        for d in range(n):
+            p = lax.rem(me + half + d, n)
+            normalise(None, turned, chunk, p)
+            if d == half:
+                keep(chunk, 0)
+            else:
+                send(chunk, p, 0)
+
+        @pl.when(j == PAIR - 1)
+        def _():
+            load((chunk + 1) // PAIR, wide, tall, load_bulk, lambda c: c.start())
+
+    def send(chunk, p, m):
+        s = m
+        if m == 2:
+            s = jnp.where(chunk >= first_held, jnp.where(chunk == 3 * experts - 1, 4, 3), 2)
+        pltpu.make_async_remote_copy(
+            stage.at[chunk, p], outs[m].at[chunk - m * experts, :, my_columns], bulk_send.at[s], bulk_recv.at[s],
+            device_id={"shard": p}, device_id_type=MESH,
+        ).start()
 
     def bulk(group):
-        message(steps - 1, group).wait_recv()
-        scales[group * PAIR + 1 - core] = got[steps - 1, group]
+        message(last, group).wait_recv()
+        scales[group * PAIR + 1 - core] = got[last, group]
+
         load(group, wide, tall, load_bulk, lambda c: c.wait())
 
         @pl.loop(0, PAIR)
         def _(j):
             chunk = group * PAIR + j
-            for b in range(inner // LANES):
-                lanes = pl.ds(b * LANES, LANES)
-                column[lanes] = jnp.broadcast_to(scales[chunk, :, lanes], (LANES, LANES)).T
+            spread(chunk)
 
             @pl.when(group < wide_groups)
             def _():
-                for b in range(inner // LANES):
-                    lanes = pl.ds(b * LANES, LANES)
-                    for h in range(depth // LANES):
-                        half = pl.ds(h * LANES, LANES)
-                        turned[lanes, half] = wide[j, half, lanes].T
-                normalise(None, turned, chunk)
+                turn_over(j)
+                for p in range(n):
+                    normalise(None, turned, chunk, p)
 
             @pl.when(group >= wide_groups)
             def _():
-                normalise(j, tall, chunk)
+                for p in range(n):
+                    normalise(j, tall, chunk, p)
 
             for m in range(3):
 
                 @pl.when(group // per_array == m)
                 def _():
-                    place = outs[m].at[chunk - m * experts, :, my_columns]
                     for d in range(n):
                         p = lax.rem(me + n // 2 + d, n)
                         if d == n // 2:
-                            pltpu.make_async_copy(stage.at[chunk, me], place, own_sem.at[m]).start()
+                            keep(chunk, m)
+                        elif m < 2 or d % CORES:
+                            send(chunk, p, m)
                         else:
-                            pltpu.make_async_remote_copy(
-                                stage.at[chunk, p], place, bulk_send.at[m], bulk_recv.at[m],
-                                device_id={"shard": p}, device_id_type=MESH,
-                            ).start()
+                            hold = (chunk >= first_held) & (p // half != me // half)
+
+                            @pl.when(jnp.logical_not(hold))
+                            def _():
+                                send(chunk, p, m)
+
+                            @pl.when(hold & (core == 0))
+                            def _():
+                                pltpu.make_async_copy(
+                                    stage.at[chunk, p], later.at[chunk - first_held, lax.rem(p, half) // CORES], later_sem
+                                ).start()
 
         @pl.when(group + 1 < total)
         def _():
             load(group + 1, wide, tall, load_bulk, lambda c: c.start())
 
-    @pl.loop(0, total + steps)
+    @pl.loop(LEAD, total + steps)
     def _(t):
         for step in reversed(range(1, steps)):
 
-            @pl.when((t >= step) & (t < total + step))
+            @pl.when((t >= step + LEAD) & (t < total + step))
             def _():
                 reduce_step(step, t - step)
 
@@ -173,7 +298,7 @@
         def _():
             local_max(t)
 
-        @pl.when(t == 1)
+        @pl.when(t == LEAD + 1)
         def _():
             pltpu.make_async_copy(router_bytes, router_bytes, router_sem.at[1]).wait()
             for d in range(1, groups_of_experts):
@@ -182,26 +307,149 @@
                     device_id={"expert": lax.rem(team + d, groups_of_experts)}, device_id_type=MESH,
                 ).start()
 
-        @pl.when(t >= steps)
+        @pl.when((t > LEAD) & (t <= LEAD + direct))
+        def _():
+            first_bulk(t - LEAD - 1)
+
+        @pl.when(t >= LEAD + steps)
         def _():
             bulk(t - steps)
+
+    def done(sems, s, m, count, width):
+        moved = outs[m].at[pl.ds(0, count), :, pl.ds(0, width * depth)]
+        pltpu.make_async_copy(moved, moved, sems.at[s]).wait()
+
+    def done_first(sems, narrow):
+        for m in range(3):
+            done(sems, m, m, experts - held if m == 2 else experts, n - 1)
+        done(sems, 3, 2, held - 1, n - 1 - narrow)
+
+    @pl.when(core == 0)
+    def _():
+        done_first(bulk_send, half // CORES)
+        for q in range(half // CORES):
+            pl.semaphore_signal(
+                turn, inc=1, device_id={"shard": me // half * half + CORES * q + 1}, device_id_type=MESH
+            )
+        done(bulk_send, 4, 2, 1, n - 1 - half // CORES)
+
+    @pl.when(core > 0)
+    def _():
+        pl.semaphore_wait(turn, half // CORES)
+
+        @pl.loop(first_held, 3 * experts)
+        def _(chunk):
+            for p in across(n, me):
+                send(chunk, p, 2)
 
     pltpu.make_async_copy(router_bytes, router_bytes, router_sem.at[0]).wait()
     for s in (2, 3):
         pltpu.make_async_copy(team_bytes, team_bytes, router_sem.at[s]).wait()
     router[...] = rows[...]
 
-    @pl.loop(0, total)
+    @pl.loop(LEAD, total)
     def _(group):
         for step in range(steps):
-            message(step, group).wait_send()
+            if step in (cross, share):
+
+                @pl.when(crosses(group))
+                def _():
+                    message(step, group).wait_send()
+            else:
+                message(step, group).wait_send()
+
+    for k in range(2):
+        pltpu.make_async_copy(first_bytes(k), first_bytes(k), first_send.at[k]).wait()
 
     for m in range(3):
-        sent = outs[m].at[:, :, pl.ds(0, (n - 1) * depth)]
         own = outs[m].at[:, :, pl.ds(0, depth)]
         pltpu.make_async_copy(own, own, own_sem.at[m]).wait()
-        pltpu.make_async_copy(sent, sent, bulk_send.at[m]).wait()
-        pltpu.make_async_copy(sent, sent, bulk_recv.at[m]).wait()
+
+    @pl.when(core == 0)
+    def _():
+        pltpu.make_async_copy(later, later, later_sem).wait()
+        done_first(bulk_recv, half // CORES)
+        done(bulk_recv, 4, 2, 1, n - 1 - half // CORES)
+
+    @pl.when(core > 0)
+    def _():
+        for sems in (bulk_send, bulk_recv):
+            done_first(sems, 0)
+            done(sems, 4, 2, 1, n - 1)
+
+
+def place(
+    gate, up, down, router, out_gate, out_up, out_down, out_router, token,
+    buffer, router_buffer, loads, stores, router_sem,
+):
+    ins, outs = (gate, up, down), (out_gate, out_up, out_down)
+    experts = gate.shape[0]
+
+    def load(m, e):
+        chunk = m * experts + e
+        return pltpu.make_async_copy(ins[m].at[e], buffer.at[chunk], loads.at[chunk])
+
+    for m in range(3):
+
+        @pl.loop(0, experts)
+        def _(e):
+            load(m, e).start()
+
+    pltpu.make_async_copy(router, router_buffer, router_sem).start()
+    for m in range(3):
+
+        @pl.loop(0, experts)
+        def _(e):
+            load(m, e).wait()
+            pltpu.make_async_copy(buffer.at[m * experts + e], outs[m].at[e], stores.at[m]).start()
+
+    pltpu.make_async_copy(router, router_buffer, router_sem).wait()
+    pltpu.make_async_copy(router_buffer, out_router, router_sem).start()
+    token[...] = jnp.zeros_like(token)
+    for m in range(3):
+        pltpu.make_async_copy(outs[m], outs[m], stores.at[m]).wait()
+    pltpu.make_async_copy(router_buffer, out_router, router_sem).wait()
+
+
+def finish(n, later, token, late, send_sem, recv_sem):
+    me = lax.axis_index("shard")
+    held, others = later.shape[:2]
+
+    @pl.when(lax.rem(me, CORES) == 0)
+    def _():
+        barrier = pltpu.get_barrier_semaphore()
+        for p in across(n, me):
+            pl.semaphore_signal(barrier, inc=1, device_id={"shard": p}, device_id_type=MESH)
+        pl.semaphore_wait(barrier, others)
+
+        @pl.loop(0, held)
+        def _(i):
+            for q, p in enumerate(across(n, me)):
+                pltpu.make_async_remote_copy(
+                    later.at[i, q], late.at[i, lax.rem(me, n // 2) // CORES], send_sem, recv_sem,
+                    device_id={"shard": p}, device_id_type=MESH,
+                ).start()
+
+        pltpu.make_async_copy(late, late, send_sem).wait()
+        pltpu.make_async_copy(late, late, recv_sem).wait()
+
+
+def patch(n, late, down, out_down, buffer, loads, store):
+    me = lax.axis_index("shard")
+    held, others, block, depth = late.shape
+    first = down.shape[0] - held
+
+    @pl.when(lax.rem(me, CORES) == 0)
+    def _():
+        for i in range(held):
+            for q in range(others):
+                pltpu.make_async_copy(late.at[i, q], buffer.at[i, q], loads.at[i, q]).start()
+        for i in range(held):
+            for q, p in enumerate(across(n, me)):
+                pltpu.make_async_copy(late.at[i, q], buffer.at[i, q], loads.at[i, q]).wait()
+                columns = pl.ds(pl.multiple_of(p * depth, depth), depth)
+                pltpu.make_async_copy(buffer.at[i, q], out_down.at[first + i, :, columns], store).start()
+        pltpu.make_async_copy(late, late, store).wait()
 
 
 def plain(master_gate, master_up, master_down, router_weight, router_gain):
@@ -246,24 +494,28 @@
         block = inner // n
         chunks = 3 * experts
         groups = chunks // PAIR
-        steps = n.bit_length()
+        steps = n.bit_length() + 1
         columns = router_weight.shape[1]
         fits = depth % LANES == 0 and inner % LANES == 0 and block % 8 == 0
-        if n < 4 or n & (n - 1) or experts % PAIR or not fits:
+        if n < 8 or n & (n - 1) or experts < (LEAD + 1) * PAIR or experts % PAIR or not fits:
             return plain(master_gate, master_up, master_down, router_weight, router_gain)
         f32, bf16 = jnp.float32, jnp.bfloat16
         dma = pltpu.SemaphoreType.DMA
         final = jax.ShapeDtypeStruct((experts, block, n * depth), bf16)
         hbm, vmem = pl.BlockSpec(memory_space=pl.ANY), pl.BlockSpec(memory_space=pltpu.VMEM)
-        gate, up, down, scales, router = pl.pallas_call(
+        held = chunks // HELD_SHARE
+        others = n // 2 // CORES
+        pieces = jax.ShapeDtypeStruct((held, others, block, depth), bf16)
+        gate, up, down, scales, router, later = pl.pallas_call(
             functools.partial(kernel, n, teams),
             out_shape=(
                 final, final, final,
                 jax.ShapeDtypeStruct((chunks, 1, inner), f32),
                 jax.ShapeDtypeStruct((teams * columns, n * depth), bf16),
+                pieces,
             ),
             in_specs=[hbm, hbm, hbm, vmem, vmem],
-            out_specs=(hbm, hbm, hbm, vmem, vmem),
+            out_specs=(hbm, hbm, hbm, vmem, vmem, hbm),
             scratch_shapes=[
                 pltpu.VMEM((PAIR, depth, inner), f32),
                 pltpu.VMEM((PAIR, inner, depth), f32),
@@ -279,7 +531,8 @@
                 pltpu.VMEM((teams * columns, n * depth), bf16),
                 dma, dma,
                 dma((steps, groups)), dma((steps, groups)),
-                dma((3,)), dma((3,)), dma((3,)), dma((4,)),
+                dma((5,)), dma((5,)), dma((3,)), dma((4,)), dma,
+                pltpu.VMEM((n, LEAD * PAIR, 1, inner), f32), dma((2,)), dma((2,)), pltpu.SemaphoreType.REGULAR,
             ],
             compiler_params=pltpu.CompilerParams(
                 collective_id=0, has_side_effects=True, vmem_limit_bytes=62 * 1024 * 1024
@@ -288,7 +541,43 @@
         mine = lax.dynamic_slice_in_dim(
             scales.reshape(3, experts, inner), lax.axis_index("shard") * block, block, axis=2
         )
-        return (gate.swapaxes(1, 2), up.swapaxes(1, 2), down, mine[0], mine[1], mine[2], router.T)
+        gate, up, down, router, token = pl.pallas_call(
+            place,
+            out_shape=(
+                final, final, final,
+                jax.ShapeDtypeStruct(router.shape, bf16),
+                jax.ShapeDtypeStruct((8, LANES), f32),
+            ),
+            in_specs=[hbm, hbm, hbm, hbm],
+            out_specs=(hbm, hbm, hbm, hbm, vmem),
+            scratch_shapes=[
+                pltpu.VMEM((chunks, block, n * depth), bf16),
+                pltpu.VMEM(router.shape, bf16),
+                dma((chunks,)), dma((3,)), dma,
+            ],
+            compiler_params=pltpu.CompilerParams(vmem_limit_bytes=62 * 1024 * 1024),
+        )(gate, up, down, router)
+        token, scale_gate, scale_up, scale_down = lax.optimization_barrier((token, mine[0], mine[1], mine[2]))
+        late = pl.pallas_call(
+            functools.partial(finish, n),
+            out_shape=pieces,
+            in_specs=[hbm, hbm],
+            out_specs=hbm,
+            scratch_shapes=[dma, dma],
+            compiler_params=pltpu.CompilerParams(
+                collective_id=1, has_side_effects=True, vmem_limit_bytes=62 * 1024 * 1024
+            ),
+        )(later, token)
+        down = pl.pallas_call(
+            functools.partial(patch, n),
+            out_shape=final,
+            in_specs=[hbm, hbm],
+            out_specs=hbm,
+            scratch_shapes=[pltpu.VMEM(pieces.shape, bf16), dma((held, others)), dma],
+            input_output_aliases={1: 0},
+            compiler_params=pltpu.CompilerParams(vmem_limit_bytes=62 * 1024 * 1024),
+        )(late, down)
+        return (gate.swapaxes(1, 2), up.swapaxes(1, 2), down, scale_gate, scale_up, scale_down, router.T)
 
     return jax.shard_map(
         body,

time: 793 us -> 779 us (0.982)
  local copies, waits for them, and re-layouts: 26.4 us -> 0.73 us
  Pallas kernels: 766 us -> 777 us
    pallas_call x0 -> x3, Pallas kernels: none -> 64.2 us  [the longest x1 38.4 us: body(): pl.pallas_call(functools.partial(finish, n), out_shape=pieces, in_specs=[...]
    pallas_call x1, Pallas kernels: 766 us -> 712 us  [body(): pl.pallas_call(functools.partial(kernel, n, teams), out_shape=(final, fin...]
    unnamed x15 -> x3, local copies, waits for them, and re-layouts: 25.7 us -> 0.02 us
where the time goes in v1:
time: 779 us; the launch traced here: 778 us
  Pallas kernels  777 us (100%)
    pallas_call x1, Pallas kernels, body(): pl.pallas_call(functools.partial(kernel, n, teams), out_shape=(final, fin...  712 us
    pallas_call x1, Pallas kernels, body(): pl.pallas_call(functools.partial(finish, n), out_shape=pieces, in_specs=[...  38.4 us
    pallas_call x1, Pallas kernels, body(): pl.pallas_call(place, out_shape=(final, final, final, jax.ShapeDtypeStruc...  23.5 us

profile of v1, /device:TPU:0, one launch (start us, length us, event | category | flops | bytes accessed | tf_op | source)
XLA Modules:
  0.0 778.0 jit_solution(10273554867362149731)
XLA Ops:
  0.6 712.4 %shard_map.108 = (bf16[16,176,2048]{2,1,0:T(8,128)(2,1)}, bf16[16,176,2048]{2,1,0:T(8,128)(2,1)}, bf16[16,176,2048]{2,1,0:T(8,128)(2,1)}, f32[48,1,1408]{2,1,0:T...) custom-call(f32[16,256,1408]{2,1,0:T(8,128)} %gate.1, f32[16,256,1408]{2,1,0:T(8,128)} %up.1, ...), custom_call_target="tpu_custom_call" | custom-call | tf_op jit(solution)/shard_map/pallas_call | solution.py:509
  713.1 0.0 copy-start
  713.1 23.5 %shard_map.109 = (bf16[16,176,2048]{2,1,0:T(8,128)(2,1)}, bf16[16,176,2048]{2,1,0:T(8,128)(2,1)}, bf16[16,176,2048]{2,1,0:T(8,128)(2,1)}, bf16[64,2048]{1,0:T(8,128)(2,1)}, f32[8,128]{1,0:T(8,128)}) custom-call(bf16[16,176,2048]{2,1,0:T(8,128)(2,1)} %get-tuple-element.22.gate, bf16[16,176,2048]{2,1,0:T(8,128)(2,1)} %get-tuple-element.23.up, ...), custom_call_target="tpu_custom_call" | custom-call | tf_op jit(solution)/shard_map/pallas_call | solution.py:544
  736.6 0.0 copy-done
  736.6 0.7 dynamic-slice_bitcast_fusion
  737.3 38.4 %shard_map.110.late = bf16[8,2,176,256]{3,2,1,0:T(8,128)(2,1)} custom-call(bf16[8,2,176,256]{3,2,1,0:T(8,128)(2,1)} %get-tuple-element.28.later, f32[8,128]{1,0:T(8,128)} %get-tuple-element.31.token), custom_call_target="tpu_custom_call" | custom-call | tf_op jit(solution)/shard_map/pallas_call | solution.py:561
  775.8 2.2 shard_map.111
  (1 shorter events, 0.0 us)
Async XLA Ops:
  713.1 23.5 %copy-start = (f32[48,1,1408]{2,1,0:T(1,128)S(1)}, f32[48,1,1408]{2,1,0:T(1,128)}, u32[]{:S(2)}) copy-start(f32[48,1,1408]{2,1,0:T(1,128)} %get-tuple-element.30) | copy-start | bytes 811012

commit v2 on v1

--- a/solution.py
+++ b/solution.py
@@ -11,13 +11,21 @@
 LANES = 128
 PAIR = 2
 CORES = 2
-HELD_SHARE = 6
+HELD_SHARE = 5
+EARLY = 2
 LEAD = 2
 
 
 def across(n, me):
     half = n // 2
     return [(1 - me // half) * half + lax.rem(me, CORES) + CORES * q for q in range(half // CORES)]
+
+
+def other(me, offset):
+    for bit in range(offset.bit_length()):
+        if offset >> bit & 1:
+            me = me + (1 - 2 * lax.rem(me // 2**bit, 2)) * 2**bit
+    return me
 
 
 def kernel(
@@ -25,7 +33,7 @@
     out_gate, out_up, out_down, scales, router, later,
     wide_max, tall_max, wide, tall, turned, column, stage, local, got, kept, part, rows,
     load_max, load_bulk, msg_send, msg_recv, bulk_send, bulk_recv, own_sem, router_sem, later_sem,
-    first, first_send, first_recv, turn,
+    first, first_load, first_send, first_recv, turn,
 ):
     me = lax.axis_index("shard")
     team = lax.axis_index("expert")
@@ -48,6 +56,9 @@
         size = {share: CORES, last: 1}.get(step, 2**step)
         return me + (1 - 2 * lax.rem(me // size, 2)) * size
 
+    far, near = list(range(half, n)), list(range(CORES, half))
+    orders = (far + near + [1, 0], near + far + [1, 0])
+
     def crosses(group):
         return lax.rem(me // CORES, 2) == lax.rem(group, 2)
 
@@ -67,7 +78,12 @@
                 first = lax.rem(group, per_array) * PAIR
                 act(pltpu.make_async_copy(ins[m].at[pl.ds(first, PAIR)], tall_buf if m == 2 else wide_buf, sem))
 
-    load(0, wide, tall, load_bulk, lambda c: c.start())
+    def load_first(part, sem):
+        return pltpu.make_async_copy(gate.at[part], wide.at[part], sem)
+
+    head, rest = pl.ds(0, 1), pl.ds(1, PAIR - 1)
+    load_first(head, load_bulk).start()
+    load_first(rest, first_load).start()
     load(1, wide_max, tall_max, load_max, lambda c: c.start())
 
     def first_max(source, j, chunk):
@@ -85,11 +101,12 @@
     def first_bytes(k):
         return first.at[pl.ds(0, n - 1), pl.ds(k, 1 if k == 0 else direct - 1)]
 
-    load(0, wide, tall, load_bulk, lambda c: c.wait())
+    load_first(head, load_bulk).wait()
     first_max(wide, 0, 0)
     pl.semaphore_wait(barrier, n + groups_of_experts - 2)
     for d in range(1, n):
         first_message(0, d).start()
+    load_first(rest, first_load).wait()
     for j in range(1, PAIR):
         first_max(wide, j, j)
     load(1, wide_max, tall_max, load_max, lambda c: c.wait())
@@ -216,13 +233,17 @@
             lanes = pl.ds(b * LANES, LANES)
             scales[chunk, :, lanes] = jnp.max(first[:, chunk, :, lanes], axis=0)
         spread(chunk)
-        for d in range(n):
-            p = lax.rem(me + half + d, n)
-            normalise(None, turned, chunk, p)
-            if d == half:
-                keep(chunk, 0)
-            else:
-                send(chunk, p, 0)
+        for c in range(CORES):
+
+            @pl.when(core == c)
+            def _():
+                for offset in orders[c]:
+                    p = other(me, offset)
+                    normalise(None, turned, chunk, p)
+                    if offset == 0:
+                        keep(chunk, 0)
+                    else:
+                        send(chunk, p, 0)
 
         @pl.when(j == PAIR - 1)
         def _():
@@ -237,6 +258,26 @@
             device_id={"shard": p}, device_id_type=MESH,
         ).start()
 
+    def deal(chunk, offset, m, c):
+        p = other(me, offset)
+        if offset == 0:
+            keep(chunk, m)
+        elif m < 2 or offset < half or offset % CORES:
+            send(chunk, p, m)
+        else:
+
+            @pl.when(chunk < first_held)
+            def _():
+                send(chunk, p, m)
+
+            if c == 0:
+
+                @pl.when(chunk >= first_held)
+                def _():
+                    pltpu.make_async_copy(
+                        stage.at[chunk, p], later.at[chunk - first_held, lax.rem(p, half) // CORES], later_sem
+                    ).start()
+
     def bulk(group):
         message(last, group).wait_recv()
         scales[group * PAIR + 1 - core] = got[last, group]
@@ -263,24 +304,12 @@
 
                 @pl.when(group // per_array == m)
                 def _():
-                    for d in range(n):
-                        p = lax.rem(me + n // 2 + d, n)
-                        if d == n // 2:
-                            keep(chunk, m)
-                        elif m < 2 or d % CORES:
-                            send(chunk, p, m)
-                        else:
-                            hold = (chunk >= first_held) & (p // half != me // half)
-
-                            @pl.when(jnp.logical_not(hold))
-                            def _():
-                                send(chunk, p, m)
-
-                            @pl.when(hold & (core == 0))
-                            def _():
-                                pltpu.make_async_copy(
-                                    stage.at[chunk, p], later.at[chunk - first_held, lax.rem(p, half) // CORES], later_sem
-                                ).start()
+                    for c in range(CORES):
+
+                        @pl.when(core == c)
+                        def _():
+                            for offset in orders[c]:
+                                deal(chunk, offset, m, c)
 
         @pl.when(group + 1 < total)
         def _():
@@ -293,6 +322,10 @@
             @pl.when((t >= step + LEAD) & (t < total + step))
             def _():
                 reduce_step(step, t - step)
+
+        @pl.when((t > LEAD) & (t <= LEAD + direct))
+        def _():
+            first_bulk(t - LEAD - 1)
 
         @pl.when(t < total)
         def _():
@@ -307,10 +340,6 @@
                     device_id={"expert": lax.rem(team + d, groups_of_experts)}, device_id_type=MESH,
                 ).start()
 
-        @pl.when((t > LEAD) & (t <= LEAD + direct))
-        def _():
-            first_bulk(t - LEAD - 1)
-
         @pl.when(t >= LEAD + steps)
         def _():
             bulk(t - steps)
@@ -327,20 +356,21 @@
     @pl.when(core == 0)
     def _():
         done_first(bulk_send, half // CORES)
+        done(bulk_send, 4, 2, 1, n - 1 - half // CORES)
         for q in range(half // CORES):
             pl.semaphore_signal(
                 turn, inc=1, device_id={"shard": me // half * half + CORES * q + 1}, device_id_type=MESH
             )
-        done(bulk_send, 4, 2, 1, n - 1 - half // CORES)
 
     @pl.when(core > 0)
     def _():
-        pl.semaphore_wait(turn, half // CORES)
-
-        @pl.loop(first_held, 3 * experts)
-        def _(chunk):
+        def send_held(chunk):
             for p in across(n, me):
                 send(chunk, p, 2)
+
+        pl.loop(first_held, first_held + EARLY)(send_held)
+        pl.semaphore_wait(turn, half // CORES)
+        pl.loop(first_held + EARLY, 3 * experts)(send_held)
 
     pltpu.make_async_copy(router_bytes, router_bytes, router_sem.at[0]).wait()
     for s in (2, 3):
@@ -532,7 +562,7 @@
                 dma, dma,
                 dma((steps, groups)), dma((steps, groups)),
                 dma((5,)), dma((5,)), dma((3,)), dma((4,)), dma,
-                pltpu.VMEM((n, LEAD * PAIR, 1, inner), f32), dma((2,)), dma((2,)), pltpu.SemaphoreType.REGULAR,
+                pltpu.VMEM((n, LEAD * PAIR, 1, inner), f32), dma, dma((2,)), dma((2,)), pltpu.SemaphoreType.REGULAR,
             ],
             compiler_params=pltpu.CompilerParams(
                 collective_id=0, has_side_effects=True, vmem_limit_bytes=62 * 1024 * 1024

time: 779 us -> 761 us (0.977)
  Pallas kernels: 777 us -> 759 us
    pallas_call x1, Pallas kernels: 712 us -> 693 us  [body(): pl.pallas_call(functools.partial(kernel, n, teams), out_shape=(final, fin...]
where the time goes in v2:
time: 761 us; the launch traced here: 760 us
  Pallas kernels  759 us (100%)
    pallas_call x1, Pallas kernels, body(): pl.pallas_call(functools.partial(kernel, n, teams), out_shape=(final, fin...  693 us
    pallas_call x1, Pallas kernels, body(): pl.pallas_call(functools.partial(finish, n), out_shape=pieces, in_specs=[...  39.9 us
    pallas_call x1, Pallas kernels, body(): pl.pallas_call(place, out_shape=(final, final, final, jax.ShapeDtypeStruc...  23.5 us

profile of v2, /device:TPU:0, one launch (start us, length us, event | category | flops | bytes accessed | tf_op | source)
XLA Modules:
  0.0 760.3 jit_solution(16537489251866071051)
XLA Ops:
  0.6 693.3 %shard_map.108 = (bf16[16,176,2048]{2,1,0:T(8,128)(2,1)}, bf16[16,176,2048]{2,1,0:T(8,128)(2,1)}, bf16[16,176,2048]{2,1,0:T(8,128)(2,1)}, f32[48,1,1408]{2,1,0:T...) custom-call(f32[16,256,1408]{2,1,0:T(8,128)} %gate.1, f32[16,256,1408]{2,1,0:T(8,128)} %up.1, ...), custom_call_target="tpu_custom_call" | custom-call | tf_op jit(solution)/shard_map/pallas_call | solution.py:539
  693.9 0.0 copy-start
  693.9 23.5 %shard_map.109 = (bf16[16,176,2048]{2,1,0:T(8,128)(2,1)}, bf16[16,176,2048]{2,1,0:T(8,128)(2,1)}, bf16[16,176,2048]{2,1,0:T(8,128)(2,1)}, bf16[64,2048]{1,0:T(8,128)(2,1)}, f32[8,128]{1,0:T(8,128)}) custom-call(bf16[16,176,2048]{2,1,0:T(8,128)(2,1)} %get-tuple-element.22.gate, bf16[16,176,2048]{2,1,0:T(8,128)(2,1)} %get-tuple-element.23.up, ...), custom_call_target="tpu_custom_call" | custom-call | tf_op jit(solution)/shard_map/pallas_call | solution.py:574
  717.4 0.0 copy-done
  717.5 0.7 dynamic-slice_bitcast_fusion
  718.2 39.9 %shard_map.110.late = bf16[9,2,176,256]{3,2,1,0:T(8,128)(2,1)} custom-call(bf16[9,2,176,256]{3,2,1,0:T(8,128)(2,1)} %get-tuple-element.28.later, f32[8,128]{1,0:T(8,128)} %get-tuple-element.31.token), custom_call_target="tpu_custom_call" | custom-call | tf_op jit(solution)/shard_map/pallas_call | solution.py:591
  758.0 2.3 shard_map.111
  (1 shorter events, 0.0 us)
Async XLA Ops:
  693.9 23.5 %copy-start = (f32[48,1,1408]{2,1,0:T(1,128)S(1)}, f32[48,1,1408]{2,1,0:T(1,128)}, u32[]{:S(2)}) copy-start(f32[48,1,1408]{2,1,0:T(1,128)} %get-tuple-element.30) | copy-start | bytes 811012

commit v3 on v2

--- a/solution.py
+++ b/solution.py
@@ -222,7 +222,10 @@
         def _():
             load(chunk // PAIR, wide, tall, load_bulk, lambda c: c.wait())
 
-        turn_over(j)
+        @pl.when(chunk > 0)
+        def _():
+            turn_over(j)
+
         for k in range(2):
 
             @pl.when(chunk == k)
@@ -315,6 +318,8 @@
         def _():
             load(group + 1, wide, tall, load_bulk, lambda c: c.start())
 
+    turn_over(0)
+
     @pl.loop(LEAD, total + steps)
     def _(t):
         for step in reversed(range(1, steps)):
@@ -464,7 +469,7 @@
         pltpu.make_async_copy(late, late, recv_sem).wait()
 
 
-def patch(n, late, down, out_down, buffer, loads, store):
+def patch(n, late, down, out_down, store):
     me = lax.axis_index("shard")
     held, others, block, depth = late.shape
     first = down.shape[0] - held
@@ -472,13 +477,9 @@
     @pl.when(lax.rem(me, CORES) == 0)
     def _():
         for i in range(held):
-            for q in range(others):
-                pltpu.make_async_copy(late.at[i, q], buffer.at[i, q], loads.at[i, q]).start()
-        for i in range(held):
             for q, p in enumerate(across(n, me)):
-                pltpu.make_async_copy(late.at[i, q], buffer.at[i, q], loads.at[i, q]).wait()
                 columns = pl.ds(pl.multiple_of(p * depth, depth), depth)
-                pltpu.make_async_copy(buffer.at[i, q], out_down.at[first + i, :, columns], store).start()
+                pltpu.make_async_copy(late.at[i, q], out_down.at[first + i, :, columns], store).start()
         pltpu.make_async_copy(late, late, store).wait()
 
 
@@ -590,23 +591,23 @@
         token, scale_gate, scale_up, scale_down = lax.optimization_barrier((token, mine[0], mine[1], mine[2]))
         late = pl.pallas_call(
             functools.partial(finish, n),
-            out_shape=pieces,
+            out_shape=pltpu.VMEM(pieces.shape, bf16),
             in_specs=[hbm, hbm],
-            out_specs=hbm,
+            out_specs=vmem,
             scratch_shapes=[dma, dma],
             compiler_params=pltpu.CompilerParams(
-                collective_id=1, has_side_effects=True, vmem_limit_bytes=62 * 1024 * 1024
+                collective_id=1, has_side_effects=True, vmem_limit_bytes=16 * 1024 * 1024
             ),
         )(later, token)
         down = pl.pallas_call(
             functools.partial(patch, n),
             out_shape=final,
-            in_specs=[hbm, hbm],
+            in_specs=[vmem, hbm],
             out_specs=hbm,
-            scratch_shapes=[pltpu.VMEM(pieces.shape, bf16), dma((held, others)), dma],
+            scratch_shapes=[dma],
             input_output_aliases={1: 0},
-            compiler_params=pltpu.CompilerParams(vmem_limit_bytes=62 * 1024 * 1024),
-        )(late, down)
+            compiler_params=pltpu.CompilerParams(vmem_limit_bytes=16 * 1024 * 1024),
+        )(pltpu.with_memory_space_constraint(late, pltpu.VMEM), down)
         return (gate.swapaxes(1, 2), up.swapaxes(1, 2), down, scale_gate, scale_up, scale_down, router.T)
 
     return jax.shard_map(

time: 761 us -> 760 us (level)
  no operation moved by 1% of the time
where the time goes in v3:
time: 760 us
  Pallas kernels  758 us (100%)
    pallas_call x1, Pallas kernels, body(): pl.pallas_call(functools.partial(kernel, n, teams), out_shape=(final, fin...  693 us
    pallas_call x1, Pallas kernels, body(): pl.pallas_call(functools.partial(finish, n), out_shape=pltpu.VMEM(pieces....  39.5 us
    pallas_call x1, Pallas kernels, body(): pl.pallas_call(place, out_shape=(final, final, final, jax.ShapeDtypeStruc...  23.6 us

profile of v3, /device:TPU:0, one launch (start us, length us, event | category | flops | bytes accessed | tf_op | source)
XLA Modules:
  0.0 759.7 jit_solution(13719134979133584203)
XLA Ops:
  0.6 693.3 %shard_map.108 = (bf16[16,176,2048]{2,1,0:T(8,128)(2,1)}, bf16[16,176,2048]{2,1,0:T(8,128)(2,1)}, bf16[16,176,2048]{2,1,0:T(8,128)(2,1)}, f32[48,1,1408]{2,1,0:T...) custom-call(f32[16,256,1408]{2,1,0:T(8,128)} %gate.1, f32[16,256,1408]{2,1,0:T(8,128)} %up.1, ...), custom_call_target="tpu_custom_call" | custom-call | tf_op jit(solution)/shard_map/pallas_call | solution.py:540
  693.9 0.0 copy-start.2
  693.9 0.0 copy-start
  693.9 23.6 %shard_map.109 = (bf16[16,176,2048]{2,1,0:T(8,128)(2,1)}, bf16[16,176,2048]{2,1,0:T(8,128)(2,1)}, bf16[16,176,2048]{2,1,0:T(8,128)(2,1)}, bf16[64,2048]{1,0:T(8,128)(2,1)}, f32[8,128]{1,0:T(8,128)}) custom-call(bf16[16,176,2048]{2,1,0:T(8,128)(2,1)} %get-tuple-element.22.gate, bf16[16,176,2048]{2,1,0:T(8,128)(2,1)} %get-tuple-element.23.up, ...), custom_call_target="tpu_custom_call" | custom-call | tf_op jit(solution)/shard_map/pallas_call | solution.py:575
  717.6 0.0 copy-done.2
  717.6 0.7 dynamic-slice_bitcast_fusion
  718.3 0.0 copy-done
  718.3 0.0 copy-start.1
  718.3 0.7 copy-done.1
  719.0 39.5 %shard_map.110.late = bf16[9,2,176,256]{3,2,1,0:T(8,128)(2,1)S(1)} custom-call(bf16[9,2,176,256]{3,2,1,0:T(8,128)(2,1)S(1)} %copy-done, f32[8,128]{1,0:T(8,128)S(1)} %copy-done.1), custom_call_target="tpu_custom_call" | custom-call | tf_op jit(solution)/shard_map/pallas_call | solution.py:592
  758.5 1.2 shard_map.111
  (1 shorter events, 0.0 us)
Async XLA Ops:
  693.9 23.7 %copy-start.2 = (f32[48,1,1408]{2,1,0:T(1,128)S(1)}, f32[48,1,1408]{2,1,0:T(1,128)}, u32[]{:S(2)}) copy-start(f32[48,1,1408]{2,1,0:T(1,128)} %get-tuple-element.30) | copy-start | bytes 811012
  693.9 24.4 %copy-start = (bf16[9,2,176,256]{3,2,1,0:T(8,128)(2,1)S(1)}, bf16[9,2,176,256]{3,2,1,0:T(8,128)(2,1)}, u32[]{:S(2)}) copy-start(bf16[9,2,176,256]{3,2,1,0:T(8,128)(2,1)} %get-tuple-element.28.later) | copy-start | bytes 4866052
  718.3 0.7 copy-start.1
